TPU v7x, 256 devices: a whole 4x4x8 slice. The times are simulated.
256 devices in a mesh: tm: 8 (over y, z_hi), height: 32 (over z_lo, x, core).
Axes of the slice: x: 4, y: 4, z: 8 (z_hi: 2, z_lo: 4; z = z_hi * 4 + z_lo), core: 2. Of those that a mesh axis runs over, the one named last changes fastest.
Arguments:
- latents: bfloat16 [2, 16, 64, 128, 512], P(None, 'tm', 'height'), may hold values from -6 to 6
- norm_gain: float32 [512], replicated, may hold values from 0.25 to 1.75
- spatial_weight: bfloat16 [3, 3, 512, 512], replicated, may hold values from -0.09375 to 0.09375
- temporal_weight: float32 [3, 512], replicated, may hold values from -3 to 3
- codebooks: bfloat16 [2, 65536, 512], P(None, 'height'), may hold values from -6 to 6
- ema_counts: float32 [2, 65536], P(None, 'height'), may hold values from 0.3 to 30
- ema_sums: float32 [2, 65536, 512], P(None, 'height', 'tm'), may hold values from -6 to 6
- decay: float32 [2], replicated, may hold values from 0.6 to 0.9
- codes_first: int32 [2, 16, 64, 128], P(None, 'tm', 'height'), may hold values from 0 to 65535, as said below
- codes_second: int32 [2, 16, 64, 128], P(None, 'tm', 'height'), may hold values from 0 to 65535, as said below
Outputs:
- ema_counts_new: float32 [2, 65536], P(None, 'height')
- ema_sums_new: float32 [2, 65536, 512], P(None, 'height', 'tm')
- error: float32 [2, 16, 64, 128], P(None, 'tm', 'height')
Inputs may be any that keep to these rules, and one draw needn't show every extreme that they name: `codes_first`: the codes of index o of height are o * 2048 to (o + 1) * 2048 - 1. In the latents of one device (all 2 clips over its 2 frames and 2 rows) at most 64 name codes of one owner o, and in every draw, for every index of tm, some owner gets exactly 64 from every device of that index. `codes_second`: as for codes_first, drawn independently.
All inputs are finite; a program needn't handle non-finite values.
Results may differ from a plain program's by a relative error of at most 0.0031.
Values may be sent and summed in bfloat16 or wider, within the bound.
No kernel may reach another device: no remote copies, remote signals or barrier semaphores. Data moves between devices by JAX's collectives and lax.ppermute only.
A program may use at most 128 MiB of HBM per device.

v0:
```python
import functools

import jax
import jax.numpy as jnp
from jax import lax
from jax.experimental import pallas as pl
from jax.experimental.pallas import tpu as pltpu
from jax.sharding import PartitionSpec as P


BOTH = ("tm", "height")
OWNERS = 32
SLABS = 8
CAP = 64
HALF = CAP // 2
PLANE = 8
ROWS = 1024
CH = 512
CHUNK = CH // SLABS
CODE_ROWS = 2048
VMEM_LIMIT = 56 * 1024 * 1024
NT = (((1,), (1,)), ((), ()))
F32 = jnp.float32
BF16 = jnp.bfloat16


def iota(shape, dim):
    return lax.broadcasted_iota(jnp.int32, shape, dim)


def params(*semantics):
    return pltpu.CompilerParams(
        vmem_limit_bytes=VMEM_LIMIT, dimension_semantics=semantics or None
    )


def cost(flops, moved):
    return pl.CostEstimate(flops=flops, transcendentals=0, bytes_accessed=moved)


def plan_kernel(z_ref, codes_ref, ids_ref, slot_ref, place_ref):
    tri = (iota((ROWS, ROWS), 0) < iota((ROWS, ROWS), 1)).astype(F32).astype(BF16)
    table = jnp.zeros((3 * OWNERS, 2 * CAP), F32)
    for sec in range(2):
        code = codes_ref[sec : sec + 1, :]
        owner = code >> 11
        local = code & (CODE_ROWS - 1)
        hot = (iota((OWNERS, ROWS), 0) == owner).astype(F32)
        ahead = jnp.dot(hot.astype(BF16), tri, preferred_element_type=F32)
        rank = jnp.sum(hot * ahead, axis=0, keepdims=True).astype(jnp.int32)
        slot_ref[sec : sec + 1, :] = owner * CAP + rank
        away = ((owner >> 3) - z_ref[0]) & 3
        inner = owner & 7
        full = jnp.where(away == 0, 0, jnp.where(away == 3, PLANE * CAP, 2 * PLANE * CAP))
        split = 3 * PLANE * CAP + (rank >> 5) * (PLANE * HALF) + inner * HALF + (rank & (HALF - 1))
        place_ref[sec : sec + 1, :] = jnp.where(away == 2, split, full + inner * CAP + rank)
        high = (local >> 6).astype(F32)
        low = (local & 63).astype(F32)
        left = jnp.concatenate([hot, hot * high, hot * low], axis=0).astype(BF16)
        right = (iota((2 * CAP, ROWS), 0) == rank + sec * CAP).astype(F32).astype(BF16)
        table = table + lax.dot_general(left, right, NT, preferred_element_type=F32)
    filled = table[:OWNERS]
    value = table[OWNERS : 2 * OWNERS] * 64.0 + table[2 * OWNERS :]
    ids_ref[...] = jnp.where(filled > 0.5, value, -1.0).astype(jnp.int32)


def make_plan(z_low, codes):
    return pl.pallas_call(
        plan_kernel,
        in_specs=[
            pl.BlockSpec(memory_space=pltpu.SMEM),
            pl.BlockSpec(memory_space=pltpu.VMEM),
        ],
        out_shape=(
            jax.ShapeDtypeStruct((OWNERS, 2 * CAP), jnp.int32),
            jax.ShapeDtypeStruct((2, ROWS), jnp.int32),
            jax.ShapeDtypeStruct((2, ROWS), jnp.int32),
        ),
        compiler_params=params(),
        cost_estimate=cost(4 * OWNERS * ROWS * ROWS, 1 << 16),
        name="plan",
    )(z_low, codes)


def columns(row):
    parts = []
    for start in range(0, row.shape[1], 128):
        piece = jnp.broadcast_to(row[:, start : start + 128], (128, 128))
        parts.append(jnp.transpose(piece))
    return jnp.concatenate(parts, axis=0)


def one_hot(cols, width, offset=0):
    lanes = iota(cols.shape, 1)
    parts = [
        (cols == lanes + (offset + start)).astype(F32).astype(BF16)
        for start in range(0, width, 128)
    ]
    return jnp.concatenate(parts, axis=1)


def serve_kernel(ids_ref, table_ref, out_ref):
    picks = one_hot(columns(ids_ref[0]), CODE_ROWS)
    got = jnp.dot(picks, table_ref[0], preferred_element_type=F32)
    out_ref[...] = got.astype(BF16).reshape(out_ref.shape)


def serve(ids, codebooks, sec):
    step = 512
    per = ids.shape[1]
    return pl.pallas_call(
        serve_kernel,
        grid=(ids.size // step,),
        in_specs=[
            pl.BlockSpec((1, 1, step), lambda i: (i, 0, 0)),
            pl.BlockSpec((1, CODE_ROWS, CH), lambda i: (sec, 0, 0)),
        ],
        out_specs=pl.BlockSpec((step // per, per, CH), lambda i: (i, 0, 0)),
        out_shape=jax.ShapeDtypeStruct((PLANE, per, CH), BF16),
        compiler_params=params("arbitrary"),
        cost_estimate=cost(2 * ids.size * CODE_ROWS * CH, 4 << 20),
        name="serve",
    )(ids.reshape(-1, 1, step), codebooks)


def picked(place_row, tables):
    cols = columns(place_row)
    got, start = None, 0
    for table in tables:
        size = table.shape[0] * table.shape[1]
        made = jnp.dot(
            one_hot(cols, size, start),
            table[...].reshape(size, CH),
            preferred_element_type=F32,
        )
        got = made if got is None else got + made
        start += size
    return got


def unpack_kernel(place_ref, *refs):
    refs[-1][...] = picked(place_ref[0], refs[:-1]).astype(BF16)


def unpack(place, tables):
    step = 512
    whole = [pl.BlockSpec(table.shape, lambda i: (0, 0, 0)) for table in tables]
    return pl.pallas_call(
        unpack_kernel,
        grid=(ROWS // step,),
        in_specs=[pl.BlockSpec((1, 1, step), lambda i: (i, 0, 0)), *whole],
        out_specs=pl.BlockSpec((step, CH), lambda i: (i, 0)),
        out_shape=jax.ShapeDtypeStruct((ROWS, CH), BF16),
        compiler_params=params("arbitrary"),
        cost_estimate=cost(2 * ROWS * CODE_ROWS * CH, 3 << 20),
        name="unpack",
    )(place.reshape(ROWS // step, 1, step), *tables)


def conv_kernel(before_ref, own_ref, after_ref, gain_ref, weight_ref, out_ref, normed_ref):
    @pl.when(pl.program_id(0) == 0)
    def _():
        def put(values, start):
            wide = values.astype(F32)
            inverse = lax.rsqrt(jnp.mean(wide * wide, axis=-1, keepdims=True) + 1e-06)
            normed_ref[:, start : start + values.shape[1], :] = (
                wide * inverse * gain_ref[...]
            ).astype(BF16)

        put(own_ref[...], 128)
        put(before_ref[...], 0)
        put(after_ref[...], 384)

    frames = normed_ref.shape[0]
    width = out_ref.shape[-1]
    column = iota((frames * 256, width), 0) & 127
    total = None
    for col in (1, 0, 2):
        part = None
        for row in range(3):
            window = normed_ref[:, row * 128 : row * 128 + 256, :].reshape(frames * 256, CH)
            made = jnp.dot(window, weight_ref[row, col], preferred_element_type=F32)
            part = made if part is None else part + made
        if col == 0:
            part = jnp.where(column == 0, 0.0, pltpu.roll(part, 1, 0))
        elif col == 2:
            part = jnp.where(column == 127, 0.0, pltpu.roll(part, frames * 256 - 1, 0))
        total = part if total is None else total + part
    out_ref[...] = (total / (1.0 + jnp.exp(-total))).astype(BF16).reshape(out_ref.shape)


def convolve(before, own, after, gain, weight):
    width = 256
    frames = own.shape[0]
    whole = lambda rows: pl.BlockSpec((frames, rows, CH), lambda i: (0, 0, 0))
    return pl.pallas_call(
        conv_kernel,
        grid=(CH // width,),
        in_specs=[
            whole(128),
            whole(256),
            whole(128),
            pl.BlockSpec((1, 1, CH), lambda i: (0, 0, 0)),
            pl.BlockSpec((3, 3, CH, width), lambda i: (0, 0, 0, i)),
        ],
        out_specs=pl.BlockSpec((frames, 256, width), lambda i: (0, 0, i)),
        out_shape=jax.ShapeDtypeStruct((frames, 256, CH), BF16),
        scratch_shapes=[pltpu.VMEM((frames, 512, CH), BF16)],
        compiler_params=params("arbitrary"),
        cost_estimate=cost(18 * ROWS * CH * CH, 8 << 20),
        name="conv",
    )(before, own, after, gain.reshape(1, 1, CH), weight)


def pack_into(turned_ref, slot_row, out_ref):
    step = 256
    left = iota((SLABS, HALF, 128), 2) < 64

    def chunk(index, carry):
        hot = (iota((step, ROWS), 0) + index * step == slot_row).astype(F32).astype(BF16)
        block = lax.dot_general(turned_ref[...], hot, NT, preferred_element_type=F32)
        for pair in range(step // 128):
            piece = block[:, pair * 128 : (pair + 1) * 128].reshape(SLABS, CHUNK, 128)
            top, low = piece[:, :HALF], piece[:, HALF:]
            owner = index * (step // CAP) + 2 * pair
            out_ref[:, owner] = jnp.where(left, top, pltpu.roll(low, 64, 2)).astype(BF16)
            out_ref[:, owner + 1] = jnp.where(left, pltpu.roll(top, 64, 2), low).astype(BF16)
        return carry

    lax.fori_loop(0, OWNERS * CAP // step, chunk, 0)


MESSAGE = jax.ShapeDtypeStruct((SLABS, OWNERS, HALF, 128), BF16)


def first_kernel(lat_ref, hid_ref, prev_ref, taps_ref, slot_ref, out_ref, enc_ref, turned_ref):
    taps = [taps_ref[tap : tap + 1, :] for tap in range(3)]
    clips, frames = lat_ref.shape[0], lat_ref.shape[1]
    for clip in range(clips):
        series = [prev_ref[clip, f].astype(F32) for f in range(frames)]
        series += [hid_ref[clip, f].astype(F32) for f in range(frames)]
        for frame in range(frames):
            mixed = taps[0] * series[frame]
            mixed = mixed + taps[1] * series[frame + 1]
            mixed = mixed + taps[2] * series[frame + 2]
            made = (lat_ref[clip, frame].astype(F32) + mixed).astype(BF16)
            start = (clip * frames + frame) * 256
            enc_ref[start : start + 256, :] = made
            turned_ref[:, start : start + 256] = jnp.transpose(made.astype(F32)).astype(BF16)
    pack_into(turned_ref, slot_ref[...], out_ref)


def pack_first(lat, hid, prev, taps, slot):
    return pl.pallas_call(
        first_kernel,
        out_shape=(MESSAGE, jax.ShapeDtypeStruct((ROWS, CH), BF16)),
        scratch_shapes=[pltpu.VMEM((CH, ROWS), BF16)],
        compiler_params=params(),
        cost_estimate=cost(2 * ROWS * CODE_ROWS * CH, 6 << 20),
        name="pack_first",
    )(lat, hid, prev, taps, slot)


def second_kernel(enc_ref, place_ref, slot_ref, *refs):
    out_ref, res_ref, turned_ref = refs[-3:]
    for start in range(0, ROWS, 512):
        quant = picked(place_ref[:, start : start + 512], refs[:-3])
        made = (enc_ref[start : start + 512, :].astype(F32) - quant).astype(BF16)
        res_ref[start : start + 512, :] = made
        turned_ref[:, start : start + 512] = jnp.transpose(made.astype(F32)).astype(BF16)
    pack_into(turned_ref, slot_ref[...], out_ref)


def pack_second(enc, place, slot, tables):
    return pl.pallas_call(
        second_kernel,
        out_shape=(MESSAGE, jax.ShapeDtypeStruct((ROWS, CH), BF16)),
        scratch_shapes=[pltpu.VMEM((CH, ROWS), BF16)],
        compiler_params=params(),
        cost_estimate=cost(4 * ROWS * CODE_ROWS * CH, 6 << 20),
        name="pack_second",
    )(enc, place, slot, *tables)


def counts_kernel(ids_ref, ema_ref, keep_ref, out_ref, acc_ref):
    step = pl.program_id(0)

    @pl.when(step == 0)
    def _():
        acc_ref[...] = jnp.zeros_like(acc_ref)

    groups = CODE_ROWS // CH
    for sec in range(2):
        hots, rows = [], []
        for pair in range(ids_ref.shape[2]):
            code = ids_ref[sec, 0, pair : pair + 1, :]
            hots.append((iota((CH, 128), 0) == (code & (CH - 1))).astype(F32).astype(BF16))
            rows.append((iota((8, 128), 0) == (code >> 9)).astype(F32).astype(BF16))
        acc_ref[sec] += lax.dot_general(
            jnp.concatenate(rows, axis=1),
            jnp.concatenate(hots, axis=1),
            NT,
            preferred_element_type=F32,
        )

    @pl.when(step == pl.num_programs(0) - 1)
    def _():
        for sec in range(2):
            keep = keep_ref[sec]
            for g in range(groups):
                span = slice(g * CH, (g + 1) * CH)
                out_ref[sec : sec + 1, span] = (
                    keep * ema_ref[sec : sec + 1, span]
                    + (1.0 - keep) * acc_ref[sec, g : g + 1, :]
                )


def new_counts(ids, ema_counts, decay):
    steps = ids.shape[1]
    whole = pl.BlockSpec((2, CODE_ROWS), lambda i: (0, 0))
    return pl.pallas_call(
        counts_kernel,
        grid=(steps,),
        in_specs=[
            pl.BlockSpec((2, 1, *ids.shape[2:]), lambda i: (0, i, 0, 0)),
            whole,
            pl.BlockSpec(memory_space=pltpu.SMEM),
        ],
        out_specs=whole,
        out_shape=jax.ShapeDtypeStruct((2, CODE_ROWS), F32),
        scratch_shapes=[pltpu.VMEM((2, 8, CH), F32)],
        compiler_params=params("arbitrary"),
        cost_estimate=cost(4 * 128 * CH * 256 * CAP, 1 << 18),
        name="counts",
    )(ids, ema_counts, decay)


def sums_kernel(sec, got_ref, ids_ref, ema_ref, decay_ref, *rest):
    out_ref, acc_ref = rest[-2:]
    step = pl.program_id(0)
    left = iota((HALF, 128), 1) < 64
    groups = CODE_ROWS // CH
    hots, wides = [], []
    for pair in range(got_ref.shape[0] // 2):
        code = ids_ref[0, 0, pair : pair + 1, :]
        group = code >> 9
        hots.append((iota((CH, 128), 0) == (code & (CH - 1))).astype(F32).astype(BF16))
        one = got_ref[2 * pair].astype(F32)
        two = got_ref[2 * pair + 1].astype(F32)
        block = jnp.concatenate(
            [
                jnp.where(left, one, pltpu.roll(two, 64, 1)),
                jnp.where(left, pltpu.roll(one, 64, 1), two),
            ],
            axis=0,
        )
        rows = [jnp.where(group == g, block, 0.0) for g in range(groups)]
        wides.append(jnp.concatenate(rows, axis=0).astype(BF16))
    hot = jnp.concatenate(hots, axis=1)
    wide = jnp.concatenate(wides, axis=1)
    made = lax.dot_general(wide, hot, NT, preferred_element_type=F32)

    @pl.when(step == 0)
    def _():
        acc_ref[...] = made

    @pl.when(step != 0)
    def _():
        acc_ref[...] += made

    @pl.when(step == pl.num_programs(0) - 1)
    def _():
        keep = decay_ref[sec]
        for g in range(groups):
            span = slice(g * CH, (g + 1) * CH)
            out_ref[0, :, span] = keep * ema_ref[0, :, span] + (1.0 - keep) * acc_ref[
                g * CHUNK : (g + 1) * CHUNK, :
            ]


def sums(sec, got, ids, ema, decay, earlier=None):
    sources = 2 * ids.shape[2]
    block = pl.BlockSpec((1, CHUNK, CODE_ROWS), lambda i: (sec, 0, 0))
    in_specs = [
        pl.BlockSpec((sources, HALF, 128), lambda i: (i, 0, 0)),
        pl.BlockSpec((1, 1, *ids.shape[2:]), lambda i: (sec, i, 0, 0)),
        block,
        pl.BlockSpec(memory_space=pltpu.SMEM),
    ]
    args = [got, ids, ema, decay]
    aliases = {}
    if earlier is not None:
        in_specs.append(pl.BlockSpec(memory_space=pl.ANY))
        args.append(earlier)
        aliases = {4: 0}
    return pl.pallas_call(
        functools.partial(sums_kernel, sec),
        grid=(got.shape[0] // sources,),
        in_specs=in_specs,
        out_specs=block,
        out_shape=jax.ShapeDtypeStruct((2, CHUNK, CODE_ROWS), F32),
        scratch_shapes=[pltpu.VMEM((CODE_ROWS // CH * CHUNK, CH), F32)],
        input_output_aliases=aliases,
        compiler_params=params("arbitrary"),
        cost_estimate=cost(2 * 256 * CH * 256 * CAP, 4 << 20),
        name="sums",
    )(*args)


def device(y, z, inner):
    return (y * 2 + z // 4) * OWNERS + (z % 4) * PLANE + inner


def along_z(x, steps):
    pairs = [
        (device(y, z, inner), device(y, (z + steps) % 8, inner))
        for y in range(4)
        for z in range(8)
        for inner in range(PLANE)
    ]
    return lax.ppermute(x, BOTH, pairs)


def in_plane(x):
    groups = [list(range(z * PLANE, (z + 1) * PLANE)) for z in range(4)]
    return lax.all_to_all(x, "height", 0, 0, axis_index_groups=groups, tiled=True)


def spread(served):
    got = in_plane(served)
    ahead, behind = got[:, CAP : 2 * CAP], got[:, 2 * CAP : 3 * CAP]
    far_ahead, far_behind = got[:, 3 * CAP : 3 * CAP + HALF], got[:, 3 * CAP + HALF :]
    moved = (along_z(ahead, 1), along_z(behind, -1), along_z(far_behind, -2), along_z(far_ahead, 2))
    return (got[:, :CAP], *moved)


def sent_to_owners(message):
    return lax.all_to_all(message.reshape(-1, HALF, 128), BOTH, 0, 0, tiled=True)


def block(
    latents,
    norm_gain,
    spatial_weight,
    temporal_weight,
    codebooks,
    ema_counts,
    ema_sums,
    decay,
    codes_first,
    codes_second,
):
    tm, height = lax.axis_index("tm"), lax.axis_index("height")
    up = [(i, i + 1) for i in range(OWNERS - 1)]
    down = [(i + 1, i) for i in range(OWNERS - 1)]
    before = lax.ppermute(latents[:, :, 1], "height", up).reshape(4, 128, CH)
    after = lax.ppermute(latents[:, :, 0], "height", down).reshape(4, 128, CH)

    codes = jnp.stack([codes_first.reshape(ROWS), codes_second.reshape(ROWS)])
    z_low = height // PLANE
    ids, slot, place = make_plan(z_low.reshape(1), codes)
    sent = jnp.broadcast_to(ids[None], (2, OWNERS, 2 * CAP)).reshape(-1, 2 * CAP)
    sheets = [list(range(y * 2 * OWNERS, (y + 1) * 2 * OWNERS)) for y in range(4)]
    asked = lax.all_to_all(sent, BOTH, 0, 0, axis_index_groups=sheets, tiled=True)

    own = latents.reshape(4, 256, CH)
    hidden = convolve(before, own, after, norm_gain, spatial_weight)
    previous = lax.ppermute(hidden, "tm", [(i, i + 1) for i in range(SLABS - 1)])
    asked, hidden = lax.optimization_barrier((asked, hidden))

    rings = [list(range(start, SLABS, 2)) for start in range(2)]
    known = lax.all_gather(asked, "tm", axis_index_groups=rings, tiled=True)
    by_z = asked.reshape(8, PLANE, 2 * CAP)
    here = (tm & 1) * 4 + z_low
    wanted = {
        step: lax.dynamic_index_in_dim(by_z, (here + step) & 7, 0, keepdims=False)
        for step in (0, 1, -1, 2, -2)
    }
    answers = []
    for sec in range(2):
        start = sec * CAP
        rows = jnp.concatenate(
            [
                wanted[0][:, start : start + CAP],
                wanted[1][:, start : start + CAP],
                wanted[-1][:, start : start + CAP],
                wanted[2][:, start + HALF : start + CAP],
                wanted[-2][:, start : start + HALF],
            ],
            axis=1,
        )
        served = serve(rows, codebooks, sec)
        answers.append(spread(served))

    clip_form = lambda x: x.reshape(2, 2, 256, CH)
    first_out, encoded = pack_first(
        clip_form(latents), clip_form(hidden), clip_form(previous), temporal_weight, slot[:1]
    )
    first_in = sent_to_owners(first_out)
    second_out, residual = pack_second(encoded, place[:1], slot[1:], answers[0])
    second_in = sent_to_owners(second_out)

    second_quant = unpack(place[1], answers[1])
    leftover = residual.astype(F32) - second_quant.astype(F32)
    error = jnp.mean(leftover * leftover, axis=-1).reshape(codes_first.shape)

    turned_ema = jnp.swapaxes(ema_sums, 1, 2)
    pair_ids = jnp.stack(
        [known[:, sec * CAP : (sec + 1) * CAP].reshape(8, 16, 128) for sec in range(2)]
    )
    ema_counts_new = new_counts(pair_ids, ema_counts, decay)
    partial = sums(0, first_in, pair_ids, turned_ema, decay)
    done = sums(1, second_in, pair_ids, turned_ema, decay, partial)
    ema_sums_new = jnp.swapaxes(done, 1, 2)
    return (ema_counts_new, ema_sums_new, error)


def solution(mesh):
    return jax.shard_map(
        block,
        mesh=mesh,
        in_specs=(
            P(None, "tm", "height", None, None),
            P(),
            P(),
            P(),
            P(None, "height", None),
            P(None, "height"),
            P(None, "height", "tm"),
            P(),
            P(None, "tm", "height", None),
            P(None, "tm", "height", None),
        ),
        out_specs=(P(None, "height"), P(None, "height", "tm"), P(None, "tm", "height", None)),
        check_vma=False,
    )
```

profile of v0, /device:TPU:1, one launch (start us, length us, event | category | flops | bytes accessed | tf_op | source)
XLA Modules:
  0.0 344.9 jit_solution(18213520461442752415)
XLA Ops:
  2.0 5.1 %collective-permute-start.1 = (bf16[2,2,128,512]{3,2,1,0:T(8,128)(2,1)S(1)}, bf16[2,2,128,512]{3,2,1,0:T(8,128)(2,1)S(1)}, u32[]{:S(2)}, u32[]{:S(2)}) collective-permute-start(bf16[2,2,128,512]{3,2,1,0:T(8,128)(2,1)S(1)} %get-tuple-element.31), channel_id=1, source_target_pairs={{1,0},{2,1},{3,2},{4,3},{5,4},{6,5},{7,6},{8,7},{9,8},{10,9},{11,1... | collective-permute-start | bytes 1572872 | tf_op jit(solution)/shard_map/ppermute | solution.py:457
  7.1 1.9 collective-permute-start
  9.7 2.3 plan.1
  13.3 12.8 %all-to-all-start = ((s32[64,1,128]{2,1,0:T(1,128)}), s32[64,1,128]{2,1,0:T(1,128)S(1)}, u32[]{:S(2)}, u32[]{:S(2)}) async-start(s32[64,1,128]{2,1,0:T(1,128)} %bitcast.3), calls=%async_computation | async-start | bytes 65536 | tf_op jit(solution)/shard_map/all_to_all | solution.py:464
  27.1 9.5 %conv.1 = bf16[4,256,512]{2,1,0:T(8,128)(2,1)} custom-call(bf16[4,128,512]{2,1,0:T(8,128)(2,1)} %bitcast.48, bf16[4,256,512]{2,1,0:T(8,128)(2,1)} %bitcast.35, bf16[4,128,512]{2,1,0:T(8,128)(2,1)} %bitcast.47, f32[1,1,512]{2,1,0:T(1,128)} %bitcast.49, bf16[3,3,512,512]{3,2,1,0:T(8,128)(2,1)} %weight_ref.1), custom_call_target="tpu_custom_call" | custom-call | flops 4831838208 | bytes 8388608 | tf_op jit(solution)/shard_map/conv/pallas_call | solution.py:196
  37.5 7.6 %serve.2 = bf16[8,256,512]{2,1,0:T(8,128)(2,1)} custom-call(s32[4,1,512]{2,1,0:T(1,128)} %reshape.63.ids_ref, bf16[2,2048,512]{2,1,0:T(8,128)(2,1)} %table_ref.3), custom_call_target="tpu_custom_call" | custom-call | flops 4294967296 | bytes 4194304 | tf_op jit(solution)/shard_map/serve/pallas_call | solution.py:111
  45.1 4.8 %all-to-all-start.1 = ((bf16[8,256,512]{2,1,0:T(8,128)(2,1)}), bf16[8,256,512]{2,1,0:T(8,128)(2,1)S(1)}, u32[]{:S(2)}, u32[]{:S(2)}) async-start(bf16[8,256,512]{2,1,0:T(8,128)(2,1)} %serve.2), calls=%async_computation.1 | async-start | bytes 4194304 | tf_op jit(solution)/shard_map/all_to_all | solution.py:426
  50.6 7.6 %serve.3 = bf16[8,256,512]{2,1,0:T(8,128)(2,1)} custom-call(s32[4,1,512]{2,1,0:T(1,128)} %reshape.66.ids_ref, bf16[2,2048,512]{2,1,0:T(8,128)(2,1)} %table_ref.3), custom_call_target="tpu_custom_call" | custom-call | flops 4294967296 | bytes 4194304 | tf_op jit(solution)/shard_map/serve/pallas_call | solution.py:111
  58.3 17.9 %all-to-all-done.1 = bf16[8,256,512]{2,1,0:T(8,128)(2,1)S(1)} async-done(((bf16[8,256,512]{2,1,0:T(8,128)(2,1)}), bf16[8,256,512]{2,1,0:T(8,128)(2,1)S(1)}, u32[]{:S(2)}, u32[]{:S(2)}) %all-to-all-start.1) | async-done | bytes 2097184 | tf_op jit(solution)/shard_map/all_to_all | solution.py:426
  76.1 1.3 copy-done
  77.5 4.5 %all-to-all-start.4 = ((bf16[8,256,512]{2,1,0:T(8,128)(2,1)}), bf16[8,256,512]{2,1,0:T(8,128)(2,1)S(1)}, u32[]{:S(2)}, u32[]{:S(2)}) async-start(bf16[8,256,512]{2,1,0:T(8,128)(2,1)} %serve.3), calls=%async_computation.4 | async-start | bytes 4194304 | tf_op jit(solution)/shard_map/all_to_all | solution.py:426
  82.0 7.2 %collective-permute-start.2 = (bf16[4,256,512]{2,1,0:T(8,128)(2,1)S(1)}, bf16[4,256,512]{2,1,0:T(8,128)(2,1)S(1)}, u32[]{:S(2)}, u32[]{:S(2)}) collective-permute-start(bf16[4,256,512]{2,1,0:T(8,128)(2,1)S(1)} %copy-done.7), channel_id=1, source_target_pairs={{0,32},{32,64},{64,96},{96,128},{128,160},{160,192},{192,224},{1,3... | collective-permute-start | bytes 3145736 | tf_op jit(solution)/shard_map/ppermute | solution.py:468
  89.8 34.0 %collective-permute-done.2 = bf16[4,256,512]{2,1,0:T(8,128)(2,1)S(1)} collective-permute-done((bf16[4,256,512]{2,1,0:T(8,128)(2,1)S(1)}, bf16[4,256,512]{2,1,0:T(8,128)(2,1)S(1)}, u32[]{:S(2)}, u32[]{:S(2)}) %collective-permute-start.2) | collective-permute-done | bytes 1048608 | tf_op jit(solution)/shard_map/ppermute | solution.py:468
  124.8 8.6 %pack_first.1 = (bf16[8,32,32,128]{3,2,1,0:T(8,128)(2,1)}, bf16[1024,512]{1,0:T(8,128)(2,1)}) custom-call(bf16[2,2,256,512]{3,2,1,0:T(8,128)(2,1)} %bitcast.36, bf16[2,2,256,512]{3,2,1,0:T(8,128)(2,1)} %bitcast.45, bf16[2,2,256,512]{3,2,1,0:T(8,128)(2,1)} %bitcast.46, f32[3,512]{1,0:T(4,128)} %taps_ref.1, s32[1,1024]{1,0:T(1,128)} %get-tuple-element.54.slot_ref), custom_call_target="tpu_custom_call" | custom-call | flops 2147483648 | bytes 6291456 | tf_op jit(solution)/shard_map/pack_first/pallas_call | solution.py:254
  133.4 24.7 %all-to-all-start.3 = ((bf16[256,32,128]{2,1,0:T(8,128)(2,1)}), bf16[256,32,128]{2,1,0:T(8,128)(2,1)}, u32[]{:S(2)}, u32[]{:S(2)}) async-start(bf16[256,32,128]{2,1,0:T(8,128)(2,1)} %bitcast.34), calls=%async_computation.3 | async-start | bytes 4194304 | tf_op jit(solution)/shard_map/all_to_all | solution.py:438
  158.2 2.3 fusion.3
  160.5 4.3 %collective-permute-start.4 = (bf16[8,64,512]{2,1,0:T(8,128)(2,1)S(1)}, bf16[8,64,512]{2,1,0:T(8,128)(2,1)S(1)}, u32[]{:S(2)}, u32[]{:S(2)}) collective-permute-start(bf16[8,64,512]{2,1,0:T(8,128)(2,1)S(1)} %get-tuple-element.28), channel_id=1, source_target_pairs={{0,56},{1,57},{2,58},{3,59},{4,60},{5,61},{6,62},{7,63},{8,0},{9,1... | collective-permute-start | bytes 1572872 | tf_op jit(solution)/shard_map/ppermute | solution.py:421
  166.1 3.6 %collective-permute-start.5 = (bf16[8,32,512]{2,1,0:T(8,128)(2,1)S(1)}, bf16[8,32,512]{2,1,0:T(8,128)(2,1)S(1)}, u32[]{:S(2)}, u32[]{:S(2)}) collective-permute-start(bf16[8,32,512]{2,1,0:T(8,128)(2,1)S(1)} %get-tuple-element.27), channel_id=1, source_target_pairs={{0,48},{1,49},{2,50},{3,51},{4,52},{5,53},{6,54},{7,55},{8,56},{9,... | collective-permute-start | bytes 786440 | tf_op jit(solution)/shard_map/ppermute | solution.py:421
  169.7 54.3 %collective-permute-done.6.refs_4_ = bf16[8,32,512]{2,1,0:T(8,128)(2,1)S(1)} collective-permute-done((bf16[8,32,512]{2,1,0:T(8,128)(2,1)S(1)}, bf16[8,32,512]{2,1,0:T(8,128)(2,1)S(1)}, u32[]{:S(2)}, u32[]{:S(2)}) %collective-permute-start.6) | collective-permute-done | bytes 262176 | tf_op jit(solution)/shard_map/ppermute | solution.py:421
  224.0 1.8 collective-permute-done.5.refs_3_
  227.0 10.1 %pack_second.1 = (bf16[8,32,32,128]{3,2,1,0:T(8,128)(2,1)}, bf16[1024,512]{1,0:T(8,128)(2,1)}) custom-call(bf16[1024,512]{1,0:T(8,128)(2,1)} %get-tuple-element.16.enc_ref, s32[1,1024]{1,0:T(1,128)} %get-tuple-element.41.place_ref, s32[1,1024]{1,0:T(1,128)} %get-tuple-element.55.slot_ref, bf16[8,64,512]{2,1,0:T(8,128)(2,1)} %get-tuple-element.30.refs_0_, ...), custom_call_target="tpu_custom_call" | custom-call | flops 4294967296 | bytes 6291456 | tf_op jit(solution)/shard_map/pack_second/pallas_call | solution.py:275
  237.1 13.6 %all-to-all-start.2 = ((bf16[256,32,128]{2,1,0:T(8,128)(2,1)}), bf16[256,32,128]{2,1,0:T(8,128)(2,1)}, u32[]{:S(2)}, u32[]{:S(2)}) async-start(bf16[256,32,128]{2,1,0:T(8,128)(2,1)} %bitcast.33), calls=%async_computation.2 | async-start | bytes 4194304 | tf_op jit(solution)/shard_map/all_to_all | solution.py:438
  250.7 12.0 %all_gather.3 = s32[256,128]{1,0:T(8,128)S(1)} all-gather(s32[64,128]{1,0:T(8,128)S(1)} %bitcast.38), channel_id=1, replica_groups={{0,64,128,192},{32,96,160,224},{1,65,129,193},{33,97,161,225},{2,66,130..., dimensions={0}, use_global_device_ids=true | all-gather | bytes 163840 | tf_op jit(solution)/shard_map/all_gather | solution.py:472
  264.0 4.5 %collective-permute-start.8 = (bf16[8,64,512]{2,1,0:T(8,128)(2,1)S(1)}, bf16[8,64,512]{2,1,0:T(8,128)(2,1)S(1)}, u32[]{:S(2)}, u32[]{:S(2)}) collective-permute-start(bf16[8,64,512]{2,1,0:T(8,128)(2,1)S(1)} %get-tuple-element.23), channel_id=1, source_target_pairs={{0,56},{1,57},{2,58},{3,59},{4,60},{5,61},{6,62},{7,63},{8,0},{9,1... | collective-permute-start | bytes 1572872 | tf_op jit(solution)/shard_map/ppermute | solution.py:421
  269.0 3.2 collective-permute-start.9
  272.1 11.2 %counts.1 = f32[2,2048]{1,0:T(2,128)} custom-call(s32[2,8,16,128]{3,2,1,0:T(8,128)} %copy-done.2, f32[2,2048]{1,0:T(2,128)} %ema_ref.1, f32[2]{0:T(128)} %decay_ref.3), custom_call_target="tpu_custom_call" | custom-call | flops 4294967296 | bytes 262144 | tf_op jit(solution)/shard_map/counts/pallas_call | solution.py:321
  283.3 33.3 %collective-permute-done.10.refs_4_ = bf16[8,32,512]{2,1,0:T(8,128)(2,1)S(1)} collective-permute-done((bf16[8,32,512]{2,1,0:T(8,128)(2,1)S(1)}, bf16[8,32,512]{2,1,0:T(8,128)(2,1)S(1)}, u32[]{:S(2)}, u32[]{:S(2)}) %collective-permute-start.10) | collective-permute-done | bytes 262176 | tf_op jit(solution)/shard_map/ppermute | solution.py:421
  316.6 1.8 collective-permute-done.9.refs_3_
  319.5 5.0 %unpack.1 = bf16[1024,512]{1,0:T(8,128)(2,1)} custom-call(s32[2,1,512]{2,1,0:T(1,128)} %bitcast.42, bf16[8,64,512]{2,1,0:T(8,128)(2,1)} %get-tuple-element.25.refs_0_, bf16[8,64,512]{2,1,0:T(8,128)(2,1)} %copy-done.14, bf16[8,64,512]{2,1,0:T(8,128)(2,1)} %copy-done.13, bf16[8,32,512]{2,1,0:T(8,128)(2,1)} %copy-done.18, bf16[8,32,512]{2,1,0:T(8,128)(2,1)} %copy-done.16), custom_call_target="tpu_custom_call" | custom-call | flops 2147483648 | bytes 3145728 | tf_op jit(solution)/shard_map/unpack/pallas_call | solution.py:148
  324.6 1.6 multiply_reduce_fusion
  326.8 9.0 %sums.2.rest_0_ = f32[2,64,2048]{2,1,0:T(8,128)} custom-call(bf16[256,32,128]{2,1,0:T(8,128)(2,1)} %all-to-all-done.3.got_ref, s32[2,8,16,128]{3,2,1,0:T(8,128)} %copy-done.2, f32[2,64,2048]{2,1,0:T(8,128)} %bitcast.43, f32[2]{0:T(128)} %decay_ref.3), custom_call_target="tpu_custom_call" | custom-call | flops 4294967296 | bytes 4194304 | tf_op jit(solution)/shard_map/sums/pallas_call | solution.py:396
  335.8 9.1 %sums.3 = f32[2,64,2048]{2,1,0:T(8,128)} custom-call(bf16[256,32,128]{2,1,0:T(8,128)(2,1)} %all-to-all-done.2.got_ref, s32[2,8,16,128]{3,2,1,0:T(8,128)} %copy-done.2, f32[2,64,2048]{2,1,0:T(8,128)} %bitcast.44, f32[2]{0:T(128)} %decay_ref.3, f32[2,64,2048]{2,1,0:T(8,128)} %sums.2.rest_0_), custom_call_target="tpu_custom_call", output_to_operand_aliasing={{}: (4, {})} | custom-call | flops 4294967296 | bytes 4194304 | tf_op jit(solution)/shard_map/sums/pallas_call | solution.py:396
  (72 shorter events, 13.4 us)
Async XLA Ops:
  0.6 8.4 %copy-start.5 = (s32[2,2,2,128]{3,2,1,0:T(2,128)S(1)}, s32[2,2,2,128]{3,2,1,0:T(2,128)}, u32[]{:S(2)}) copy-start(s32[2,2,2,128]{3,2,1,0:T(2,128)} %param.19) | copy-start | bytes 12292
  0.6 8.4 %copy-start.6 = (s32[2,2,2,128]{3,2,1,0:T(2,128)S(1)}, s32[2,2,2,128]{3,2,1,0:T(2,128)}, u32[]{:S(2)}) copy-start(s32[2,2,2,128]{3,2,1,0:T(2,128)} %param.18) | copy-start | bytes 12292
  2.0 24.2 %collective-permute-start.1 = (bf16[2,2,128,512]{3,2,1,0:T(8,128)(2,1)S(1)}, bf16[2,2,128,512]{3,2,1,0:T(8,128)(2,1)S(1)}, u32[]{:S(2)}, u32[]{:S(2)}) collective-permute-start(bf16[2,2,128,512]{3,2,1,0:T(8,128)(2,1)S(1)} %get-tuple-element.31), channel_id=1, source_target_pairs={{1,0},{2,1},{3,2},{4,3},{5,4},{6,5},{7,6},{8,7},{9,8},{10,9},{11,1... | collective-permute-start | bytes 1572872 | tf_op jit(solution)/shard_map/ppermute | solution.py:457
  7.1 19.1 %collective-permute-start = (bf16[2,2,128,512]{3,2,1,0:T(8,128)(2,1)S(1)}, bf16[2,2,128,512]{3,2,1,0:T(8,128)(2,1)S(1)}, u32[]{:S(2)}, u32[]{:S(2)}) collective-permute-start(bf16[2,2,128,512]{3,2,1,0:T(8,128)(2,1)S(1)} %get-tuple-element.32), channel_id=1, source_target_pairs={{0,1},{1,2},{2,3},{3,4},{4,5},{5,6},{6,7},{7,8},{8,9},{9,10},{10,1... | collective-permute-start | bytes 1572872 | tf_op jit(solution)/shard_map/ppermute | solution.py:456
  13.3 23.3 %all-to-all-start = ((s32[64,1,128]{2,1,0:T(1,128)}), s32[64,1,128]{2,1,0:T(1,128)S(1)}, u32[]{:S(2)}, u32[]{:S(2)}) async-start(s32[64,1,128]{2,1,0:T(1,128)} %bitcast.3), calls=%async_computation | async-start | bytes 65536 | tf_op jit(solution)/shard_map/all_to_all | solution.py:464
  26.2 1.0 copy-start.10
  45.1 31.0 %all-to-all-start.1 = ((bf16[8,256,512]{2,1,0:T(8,128)(2,1)}), bf16[8,256,512]{2,1,0:T(8,128)(2,1)S(1)}, u32[]{:S(2)}, u32[]{:S(2)}) async-start(bf16[8,256,512]{2,1,0:T(8,128)(2,1)} %serve.2), calls=%async_computation.1 | async-start | bytes 4194304 | tf_op jit(solution)/shard_map/all_to_all | solution.py:426
  58.3 23.7 %copy-start.7 = (bf16[4,256,512]{2,1,0:T(8,128)(2,1)S(1)}, bf16[4,256,512]{2,1,0:T(8,128)(2,1)}, u32[]{:S(2)}) copy-start(bf16[4,256,512]{2,1,0:T(8,128)(2,1)} %conv.1) | copy-start | bytes 3145732
  58.3 30.9 %copy-start.3 = (s32[2,1024]{1,0:T(2,128)S(1)}, s32[2,1024]{1,0:T(2,128)}, u32[]{:S(2)}) copy-start(s32[2,1024]{1,0:T(2,128)} %get-tuple-element.15) | copy-start | bytes 24580
  58.3 30.9 %copy-start.4 = (s32[2,1024]{1,0:T(2,128)S(1)}, s32[2,1024]{1,0:T(2,128)}, u32[]{:S(2)}) copy-start(s32[2,1024]{1,0:T(2,128)} %get-tuple-element.17) | copy-start | bytes 24580
  76.1 1.3 copy-start
  77.5 55.9 %all-to-all-start.4 = ((bf16[8,256,512]{2,1,0:T(8,128)(2,1)}), bf16[8,256,512]{2,1,0:T(8,128)(2,1)S(1)}, u32[]{:S(2)}, u32[]{:S(2)}) async-start(bf16[8,256,512]{2,1,0:T(8,128)(2,1)} %serve.3), calls=%async_computation.4 | async-start | bytes 4194304 | tf_op jit(solution)/shard_map/all_to_all | solution.py:426
  82.0 41.9 %collective-permute-start.2 = (bf16[4,256,512]{2,1,0:T(8,128)(2,1)S(1)}, bf16[4,256,512]{2,1,0:T(8,128)(2,1)S(1)}, u32[]{:S(2)}, u32[]{:S(2)}) collective-permute-start(bf16[4,256,512]{2,1,0:T(8,128)(2,1)S(1)} %copy-done.7), channel_id=1, source_target_pairs={{0,32},{32,64},{64,96},{96,128},{128,160},{160,192},{192,224},{1,3... | collective-permute-start | bytes 3145736 | tf_op jit(solution)/shard_map/ppermute | solution.py:468
  123.8 1.0 copy-start.8
  133.4 103.7 %all-to-all-start.3 = ((bf16[256,32,128]{2,1,0:T(8,128)(2,1)}), bf16[256,32,128]{2,1,0:T(8,128)(2,1)}, u32[]{:S(2)}, u32[]{:S(2)}) async-start(bf16[256,32,128]{2,1,0:T(8,128)(2,1)} %bitcast.34), calls=%async_computation.3 | async-start | bytes 4194304 | tf_op jit(solution)/shard_map/all_to_all | solution.py:438
  160.5 65.4 %collective-permute-start.4 = (bf16[8,64,512]{2,1,0:T(8,128)(2,1)S(1)}, bf16[8,64,512]{2,1,0:T(8,128)(2,1)S(1)}, u32[]{:S(2)}, u32[]{:S(2)}) collective-permute-start(bf16[8,64,512]{2,1,0:T(8,128)(2,1)S(1)} %get-tuple-element.28), channel_id=1, source_target_pairs={{0,56},{1,57},{2,58},{3,59},{4,60},{5,61},{6,62},{7,63},{8,0},{9,1... | collective-permute-start | bytes 1572872 | tf_op jit(solution)/shard_map/ppermute | solution.py:421
  164.8 61.1 %collective-permute-start.3 = (bf16[8,64,512]{2,1,0:T(8,128)(2,1)S(1)}, bf16[8,64,512]{2,1,0:T(8,128)(2,1)S(1)}, u32[]{:S(2)}, u32[]{:S(2)}) collective-permute-start(bf16[8,64,512]{2,1,0:T(8,128)(2,1)S(1)} %get-tuple-element.29), channel_id=1, source_target_pairs={{0,8},{1,9},{2,10},{3,11},{4,12},{5,13},{6,14},{7,15},{8,16},{9,17... | collective-permute-start | bytes 1572872 | tf_op jit(solution)/shard_map/ppermute | solution.py:421
  165.9 58.2 %collective-permute-start.6 = (bf16[8,32,512]{2,1,0:T(8,128)(2,1)S(1)}, bf16[8,32,512]{2,1,0:T(8,128)(2,1)S(1)}, u32[]{:S(2)}, u32[]{:S(2)}) collective-permute-start(bf16[8,32,512]{2,1,0:T(8,128)(2,1)S(1)} %get-tuple-element.26), channel_id=1, source_target_pairs={{0,16},{1,17},{2,18},{3,19},{4,20},{5,21},{6,22},{7,23},{8,24},{9,... | collective-permute-start | bytes 786440 | tf_op jit(solution)/shard_map/ppermute | solution.py:421
  166.1 59.7 %collective-permute-start.5 = (bf16[8,32,512]{2,1,0:T(8,128)(2,1)S(1)}, bf16[8,32,512]{2,1,0:T(8,128)(2,1)S(1)}, u32[]{:S(2)}, u32[]{:S(2)}) collective-permute-start(bf16[8,32,512]{2,1,0:T(8,128)(2,1)S(1)} %get-tuple-element.27), channel_id=1, source_target_pairs={{0,48},{1,49},{2,50},{3,51},{4,52},{5,53},{6,54},{7,55},{8,56},{9,... | collective-permute-start | bytes 786440 | tf_op jit(solution)/shard_map/ppermute | solution.py:421
  224.0 1.8 copy-start.15
  225.8 0.9 copy-start.11
  225.8 1.1 copy-start.12
  237.1 98.7 %all-to-all-start.2 = ((bf16[256,32,128]{2,1,0:T(8,128)(2,1)}), bf16[256,32,128]{2,1,0:T(8,128)(2,1)}, u32[]{:S(2)}, u32[]{:S(2)}) async-start(bf16[256,32,128]{2,1,0:T(8,128)(2,1)} %bitcast.33), calls=%async_computation.2 | async-start | bytes 4194304 | tf_op jit(solution)/shard_map/all_to_all | solution.py:438
  263.0 5.5 %copy-start.2 = (s32[2,8,16,128]{3,2,1,0:T(8,128)}, s32[2,8,16,128]{3,2,1,0:T(8,128)S(1)}, u32[]{:S(2)}) copy-start(s32[2,8,16,128]{3,2,1,0:T(8,128)S(1)} %constant_dynamic-update-slice_fusion.ids_ref) | copy-start | bytes 393220
  264.0 54.4 %collective-permute-start.8 = (bf16[8,64,512]{2,1,0:T(8,128)(2,1)S(1)}, bf16[8,64,512]{2,1,0:T(8,128)(2,1)S(1)}, u32[]{:S(2)}, u32[]{:S(2)}) collective-permute-start(bf16[8,64,512]{2,1,0:T(8,128)(2,1)S(1)} %get-tuple-element.23), channel_id=1, source_target_pairs={{0,56},{1,57},{2,58},{3,59},{4,60},{5,61},{6,62},{7,63},{8,0},{9,1... | collective-permute-start | bytes 1572872 | tf_op jit(solution)/shard_map/ppermute | solution.py:421
  268.4 50.0 %collective-permute-start.7 = (bf16[8,64,512]{2,1,0:T(8,128)(2,1)S(1)}, bf16[8,64,512]{2,1,0:T(8,128)(2,1)S(1)}, u32[]{:S(2)}, u32[]{:S(2)}) collective-permute-start(bf16[8,64,512]{2,1,0:T(8,128)(2,1)S(1)} %get-tuple-element.24), channel_id=1, source_target_pairs={{0,8},{1,9},{2,10},{3,11},{4,12},{5,13},{6,14},{7,15},{8,16},{9,17... | collective-permute-start | bytes 1572872 | tf_op jit(solution)/shard_map/ppermute | solution.py:421
  268.5 48.1 %collective-permute-start.10 = (bf16[8,32,512]{2,1,0:T(8,128)(2,1)S(1)}, bf16[8,32,512]{2,1,0:T(8,128)(2,1)S(1)}, u32[]{:S(2)}, u32[]{:S(2)}) collective-permute-start(bf16[8,32,512]{2,1,0:T(8,128)(2,1)S(1)} %get-tuple-element.21), channel_id=1, source_target_pairs={{0,16},{1,17},{2,18},{3,19},{4,20},{5,21},{6,22},{7,23},{8,24},{9,... | collective-permute-start | bytes 786440 | tf_op jit(solution)/shard_map/ppermute | solution.py:421
  269.0 49.4 %collective-permute-start.9 = (bf16[8,32,512]{2,1,0:T(8,128)(2,1)S(1)}, bf16[8,32,512]{2,1,0:T(8,128)(2,1)S(1)}, u32[]{:S(2)}, u32[]{:S(2)}) collective-permute-start(bf16[8,32,512]{2,1,0:T(8,128)(2,1)S(1)} %get-tuple-element.22), channel_id=1, source_target_pairs={{0,48},{1,49},{2,50},{3,51},{4,52},{5,53},{6,54},{7,55},{8,56},{9,... | collective-permute-start | bytes 786440 | tf_op jit(solution)/shard_map/ppermute | solution.py:421
  316.6 1.8 copy-start.16
  318.4 0.9 copy-start.13
  318.4 1.1 copy-start.14
  319.5 5.0 %copy-start.1 = (bf16[1024,512]{1,0:T(8,128)(2,1)S(1)}, bf16[1024,512]{1,0:T(8,128)(2,1)}, u32[]{:S(2)}) copy-start(bf16[1024,512]{1,0:T(8,128)(2,1)} %get-tuple-element.20) | copy-start | bytes 3145732
  (3 other events, 2.2 us)
where the time goes:
time: 348 us; the launch traced here: 345 us
  waiting for transfers between devices  143 us (41%)
  starting transfers between devices  90.8 us (26%)
  Pallas kernels  80.1 us (23%)
  local copies, waits for them, and re-layouts  15.1 us (4%)
  blocking collectives  12 us (3%)
    ppermute x8, waiting for transfers between devices, along_z(): return lax.ppermute(x, BOTH, pairs)  91.2 us
    all_to_all x2, starting transfers between devices, sent_to_owners(): lax.all_to_all(message.reshape(-1, HALF, 128), BOTH, 0, 0, tiled=True)  38.3 us
    ppermute x1, waiting for transfers between devices, block(): lax.ppermute(hidden, 'tm', [(i, i + 1) for i in range(SLABS - 1)])  34 us
    pallas_call x2, Pallas kernels, sums(): pl.pallas_call(functools.partial(sums_kernel, sec), grid=(got.shape[0] //...  18.1 us
    all_to_all x2, waiting for transfers between devices, in_plane(): lax.all_to_all(x, 'height', 0, 0, axis_index_groups=groups, tiled=True)  17.9 us
    ppermute x8, starting transfers between devices, along_z(): return lax.ppermute(x, BOTH, pairs)  16.2 us
    pallas_call x2, Pallas kernels, serve(): pl.pallas_call(serve_kernel, grid=(ids.size // step,), in_specs=[pl.Block...  15.2 us
    all_to_all x1, starting transfers between devices, block(): lax.all_to_all(sent, BOTH, 0, 0, axis_index_groups=sheets, tiled=True)  12.8 us
  transfers between devices with their start and end apart: 16, of which 6 were waited for; matrix products, arithmetic and copies ran while one was open for 3% of the time, Pallas kernels for 18%

commit v1 on v0

--- a/solution.py
+++ b/solution.py
@@ -50,7 +50,7 @@
         rank = jnp.sum(hot * ahead, axis=0, keepdims=True).astype(jnp.int32)
         slot_ref[sec : sec + 1, :] = owner * CAP + rank
         away = ((owner >> 3) - z_ref[0]) & 3
-        inner = owner & 7
+        inner = (owner & 7) ^ (z_ref[1] if sec else 0)
         full = jnp.where(away == 0, 0, jnp.where(away == 3, PLANE * CAP, 2 * PLANE * CAP))
         split = 3 * PLANE * CAP + (rank >> 5) * (PLANE * HALF) + inner * HALF + (rank & (HALF - 1))
         place_ref[sec : sec + 1, :] = jnp.where(away == 2, split, full + inner * CAP + rank)
@@ -426,8 +426,19 @@
     return lax.all_to_all(x, "height", 0, 0, axis_index_groups=groups, tiled=True)
 
 
-def spread(served):
-    got = in_plane(served)
+def in_plane_apart(x, inner):
+    parts = [lax.dynamic_slice_in_dim(x, inner, 1, 0)]
+    for k in range(1, PLANE):
+        pairs = [(z + i, z + (i ^ k)) for z in range(0, OWNERS, PLANE) for i in range(PLANE)]
+        piece = lax.dynamic_slice_in_dim(x, inner ^ k, 1, 0)
+        parts.append(lax.ppermute(piece, "height", pairs))
+    return parts
+
+
+def spread(served, sec, inner):
+    got = in_plane(served) if sec == 0 else in_plane_apart(served, inner)
+    if sec == 1:
+        got = jnp.concatenate(got, axis=0)
     ahead, behind = got[:, CAP : 2 * CAP], got[:, 2 * CAP : 3 * CAP]
     far_ahead, far_behind = got[:, 3 * CAP : 3 * CAP + HALF], got[:, 3 * CAP + HALF :]
     moved = (along_z(ahead, 1), along_z(behind, -1), along_z(far_behind, -2), along_z(far_ahead, 2))
@@ -457,8 +468,8 @@
     after = lax.ppermute(latents[:, :, 0], "height", down).reshape(4, 128, CH)
 
     codes = jnp.stack([codes_first.reshape(ROWS), codes_second.reshape(ROWS)])
-    z_low = height // PLANE
-    ids, slot, place = make_plan(z_low.reshape(1), codes)
+    z_low, inner = height // PLANE, height % PLANE
+    ids, slot, place = make_plan(jnp.stack([z_low, inner]), codes)
     sent = jnp.broadcast_to(ids[None], (2, OWNERS, 2 * CAP)).reshape(-1, 2 * CAP)
     sheets = [list(range(y * 2 * OWNERS, (y + 1) * 2 * OWNERS)) for y in range(4)]
     asked = lax.all_to_all(sent, BOTH, 0, 0, axis_index_groups=sheets, tiled=True)
@@ -490,7 +501,7 @@
             axis=1,
         )
         served = serve(rows, codebooks, sec)
-        answers.append(spread(served))
+        answers.append(spread(served, sec, inner))
 
     clip_form = lambda x: x.reshape(2, 2, 256, CH)
     first_out, encoded = pack_first(

time: 348 us -> 336 us (0.966)
  waiting for transfers between devices: 143 us -> 124 us
  starting transfers between devices: 90.8 us -> 96.2 us
    ppermute x8, waiting for transfers between devices: 91.2 us -> 66.4 us  [along_z(): return lax.ppermute(x, BOTH, pairs)]
    ppermute x0 -> x7, waiting for transfers between devices: none -> 21.2 us  [in_plane_apart(): parts.append(lax.ppermute(piece, 'height', pairs))]
    all_to_all x2 -> x1, waiting for transfers between devices: 17.9 us -> 0.01 us  [in_plane(): lax.all_to_all(x, 'height', 0, 0, axis_index_groups=groups, tiled=True)]
    ppermute x0 -> x7, starting transfers between devices: none -> 14.2 us  [in_plane_apart(): parts.append(lax.ppermute(piece, 'height', pairs))]
    all_to_all x2 -> x1, starting transfers between devices: 9.27 us -> 4.94 us  [in_plane(): lax.all_to_all(x, 'height', 0, 0, axis_index_groups=groups, tiled=True)]
  transfers between devices with their start and end apart: 16 -> 22, of which waited for: 6 -> 10; matrix products, arithmetic and copies ran while one was open for 3% -> 4% of each run, Pallas kernels for 18% -> 19%
where the time goes in v1:
time: 336 us; the launch traced here: 333 us
  waiting for transfers between devices  124 us (37%)
  starting transfers between devices  96.2 us (29%)
  Pallas kernels  80.2 us (24%)
  local copies, waits for them, and re-layouts  17.1 us (5%)
  blocking collectives  10.8 us (3%)
  other arithmetic  3.45 us (1%)
    ppermute x8, waiting for transfers between devices, along_z(): return lax.ppermute(x, BOTH, pairs)  66.4 us
    ppermute x1, waiting for transfers between devices, block(): lax.ppermute(hidden, 'tm', [(i, i + 1) for i in range(SLABS - 1)])  36.4 us
    all_to_all x2, starting transfers between devices, sent_to_owners(): lax.all_to_all(message.reshape(-1, HALF, 128), BOTH, 0, 0, tiled=True)  35.9 us
    ppermute x7, waiting for transfers between devices, in_plane_apart(): parts.append(lax.ppermute(piece, 'height', pairs))  21.2 us
    pallas_call x2, Pallas kernels, sums(): pl.pallas_call(functools.partial(sums_kernel, sec), grid=(got.shape[0] //...  18.2 us
    pallas_call x2, Pallas kernels, serve(): pl.pallas_call(serve_kernel, grid=(ids.size // step,), in_specs=[pl.Block...  15.3 us
    ppermute x7, starting transfers between devices, in_plane_apart(): parts.append(lax.ppermute(piece, 'height', pairs))  14.2 us
    ppermute x8, starting transfers between devices, along_z(): return lax.ppermute(x, BOTH, pairs)  14.2 us
  transfers between devices with their start and end apart: 22, of which 10 were waited for; matrix products, arithmetic and copies ran while one was open for 4% of the time, Pallas kernels for 19%

profile of v1, /device:TPU:1, one launch (start us, length us, event | category | flops | bytes accessed | tf_op | source)
XLA Modules:
  0.0 332.8 jit_solution(8836248698869158392)
XLA Ops:
  2.0 5.1 %collective-permute-start.1 = (bf16[2,2,128,512]{3,2,1,0:T(8,128)(2,1)S(1)}, bf16[2,2,128,512]{3,2,1,0:T(8,128)(2,1)S(1)}, u32[]{:S(2)}, u32[]{:S(2)}) collective-permute-start(bf16[2,2,128,512]{3,2,1,0:T(8,128)(2,1)S(1)} %get-tuple-element.39), channel_id=1, source_target_pairs={{1,0},{2,1},{3,2},{4,3},{5,4},{6,5},{7,6},{8,7},{9,8},{10,9},{11,1... | collective-permute-start | bytes 1572872 | tf_op jit(solution)/shard_map/ppermute | solution.py:468
  10.3 2.4 plan.1
  13.9 12.8 %all-to-all-start = ((s32[64,1,128]{2,1,0:T(1,128)}), s32[64,1,128]{2,1,0:T(1,128)S(1)}, u32[]{:S(2)}, u32[]{:S(2)}) async-start(s32[64,1,128]{2,1,0:T(1,128)} %bitcast.4), calls=%async_computation | async-start | bytes 65536 | tf_op jit(solution)/shard_map/all_to_all | solution.py:475
  27.8 9.5 %conv.1 = bf16[4,256,512]{2,1,0:T(8,128)(2,1)} custom-call(bf16[4,128,512]{2,1,0:T(8,128)(2,1)} %bitcast.49, bf16[4,256,512]{2,1,0:T(8,128)(2,1)} %bitcast.36, bf16[4,128,512]{2,1,0:T(8,128)(2,1)} %bitcast.48, f32[1,1,512]{2,1,0:T(1,128)} %bitcast.50, bf16[3,3,512,512]{3,2,1,0:T(8,128)(2,1)} %weight_ref.1), custom_call_target="tpu_custom_call" | custom-call | flops 4831838208 | bytes 8388608 | tf_op jit(solution)/shard_map/conv/pallas_call | solution.py:196
  38.1 7.6 %serve.2 = bf16[8,256,512]{2,1,0:T(8,128)(2,1)} custom-call(s32[4,1,512]{2,1,0:T(1,128)} %reshape.59.ids_ref, bf16[2,2048,512]{2,1,0:T(8,128)(2,1)} %table_ref.3), custom_call_target="tpu_custom_call" | custom-call | flops 4294967296 | bytes 4194304 | tf_op jit(solution)/shard_map/serve/pallas_call | solution.py:111
  45.8 4.9 %all-to-all-start.1 = ((bf16[8,256,512]{2,1,0:T(8,128)(2,1)}), bf16[8,256,512]{2,1,0:T(8,128)(2,1)S(1)}, u32[]{:S(2)}, u32[]{:S(2)}) async-start(bf16[8,256,512]{2,1,0:T(8,128)(2,1)} %serve.2), calls=%async_computation.1 | async-start | bytes 4194304 | tf_op jit(solution)/shard_map/all_to_all | solution.py:426
  50.7 7.2 %collective-permute-start.2 = (bf16[4,256,512]{2,1,0:T(8,128)(2,1)S(1)}, bf16[4,256,512]{2,1,0:T(8,128)(2,1)S(1)}, u32[]{:S(2)}, u32[]{:S(2)}) collective-permute-start(bf16[4,256,512]{2,1,0:T(8,128)(2,1)S(1)} %copy-done.5), channel_id=1, source_target_pairs={{0,32},{32,64},{64,96},{96,128},{128,160},{160,192},{192,224},{1,3... | collective-permute-start | bytes 3145736 | tf_op jit(solution)/shard_map/ppermute | solution.py:479
  58.5 36.4 %collective-permute-done.2 = bf16[4,256,512]{2,1,0:T(8,128)(2,1)S(1)} collective-permute-done((bf16[4,256,512]{2,1,0:T(8,128)(2,1)S(1)}, bf16[4,256,512]{2,1,0:T(8,128)(2,1)S(1)}, u32[]{:S(2)}, u32[]{:S(2)}) %collective-permute-start.2) | collective-permute-done | bytes 1048608 | tf_op jit(solution)/shard_map/ppermute | solution.py:479
  95.9 8.6 %pack_first.1 = (bf16[8,32,32,128]{3,2,1,0:T(8,128)(2,1)}, bf16[1024,512]{1,0:T(8,128)(2,1)}) custom-call(bf16[2,2,256,512]{3,2,1,0:T(8,128)(2,1)} %bitcast.37, bf16[2,2,256,512]{3,2,1,0:T(8,128)(2,1)} %bitcast.46, bf16[2,2,256,512]{3,2,1,0:T(8,128)(2,1)} %bitcast.47, f32[3,512]{1,0:T(4,128)} %taps_ref.1, s32[1,1024]{1,0:T(1,128)} %get-tuple-element.62.slot_ref), custom_call_target="tpu_custom_call" | custom-call | flops 2147483648 | bytes 6291456 | tf_op jit(solution)/shard_map/pack_first/pallas_call | solution.py:254
  104.5 22.3 %all-to-all-start.3 = ((bf16[256,32,128]{2,1,0:T(8,128)(2,1)}), bf16[256,32,128]{2,1,0:T(8,128)(2,1)}, u32[]{:S(2)}, u32[]{:S(2)}) async-start(bf16[256,32,128]{2,1,0:T(8,128)(2,1)} %bitcast.35), calls=%async_computation.3 | async-start | bytes 4194304 | tf_op jit(solution)/shard_map/all_to_all | solution.py:449
  127.8 4.3 %collective-permute-start.4 = (bf16[8,64,512]{2,1,0:T(8,128)(2,1)S(1)}, bf16[8,64,512]{2,1,0:T(8,128)(2,1)S(1)}, u32[]{:S(2)}, u32[]{:S(2)}) collective-permute-start(bf16[8,64,512]{2,1,0:T(8,128)(2,1)S(1)} %get-tuple-element.36), channel_id=1, source_target_pairs={{0,56},{1,57},{2,58},{3,59},{4,60},{5,61},{6,62},{7,63},{8,0},{9,1... | collective-permute-start | bytes 1572872 | tf_op jit(solution)/shard_map/ppermute | solution.py:421
  132.2 3.6 %collective-permute-start.5 = (bf16[8,32,512]{2,1,0:T(8,128)(2,1)S(1)}, bf16[8,32,512]{2,1,0:T(8,128)(2,1)S(1)}, u32[]{:S(2)}, u32[]{:S(2)}) collective-permute-start(bf16[8,32,512]{2,1,0:T(8,128)(2,1)S(1)} %get-tuple-element.35), channel_id=1, source_target_pairs={{0,48},{1,49},{2,50},{3,51},{4,52},{5,53},{6,54},{7,55},{8,56},{9,... | collective-permute-start | bytes 786440 | tf_op jit(solution)/shard_map/ppermute | solution.py:421
  135.8 56.9 %collective-permute-done.6.refs_4_ = bf16[8,32,512]{2,1,0:T(8,128)(2,1)S(1)} collective-permute-done((bf16[8,32,512]{2,1,0:T(8,128)(2,1)S(1)}, bf16[8,32,512]{2,1,0:T(8,128)(2,1)S(1)}, u32[]{:S(2)}, u32[]{:S(2)}) %collective-permute-start.6) | collective-permute-done | bytes 262176 | tf_op jit(solution)/shard_map/ppermute | solution.py:421
  195.6 10.2 %pack_second.1 = (bf16[8,32,32,128]{3,2,1,0:T(8,128)(2,1)}, bf16[1024,512]{1,0:T(8,128)(2,1)}) custom-call(bf16[1024,512]{1,0:T(8,128)(2,1)} %get-tuple-element.16.enc_ref, s32[1,1024]{1,0:T(1,128)} %get-tuple-element.49.place_ref, s32[1,1024]{1,0:T(1,128)} %get-tuple-element.63.slot_ref, bf16[8,64,512]{2,1,0:T(8,128)(2,1)} %get-tuple-element.38.refs_0_, ...), custom_call_target="tpu_custom_call" | custom-call | flops 4294967296 | bytes 6291456 | tf_op jit(solution)/shard_map/pack_second/pallas_call | solution.py:275
  205.8 13.6 %all-to-all-start.2 = ((bf16[256,32,128]{2,1,0:T(8,128)(2,1)}), bf16[256,32,128]{2,1,0:T(8,128)(2,1)}, u32[]{:S(2)}, u32[]{:S(2)}) async-start(bf16[256,32,128]{2,1,0:T(8,128)(2,1)} %bitcast.34), calls=%async_computation.2 | async-start | bytes 4194304 | tf_op jit(solution)/shard_map/all_to_all | solution.py:449
  220.1 7.7 %serve.3 = bf16[8,256,512]{2,1,0:T(8,128)(2,1)} custom-call(s32[4,1,512]{2,1,0:T(1,128)} %reshape.62.ids_ref, bf16[2,2048,512]{2,1,0:T(8,128)(2,1)} %table_ref.3), custom_call_target="tpu_custom_call" | custom-call | flops 4294967296 | bytes 4194304 | tf_op jit(solution)/shard_map/serve/pallas_call | solution.py:111
  227.8 2.5 constant_dynamic-slice_fusion
  232.5 10.8 %all_gather.3 = s32[256,128]{1,0:T(8,128)S(1)} all-gather(s32[64,128]{1,0:T(8,128)S(1)} %bitcast.39), channel_id=1, replica_groups={{0,64,128,192},{32,96,160,224},{1,65,129,193},{33,97,161,225},{2,66,130..., dimensions={0}, use_global_device_ids=true | all-gather | bytes 163840 | tf_op jit(solution)/shard_map/all_gather | solution.py:483
  244.3 3.5 %collective-permute-start.13 = (bf16[1,256,512]{2,1,0:T(8,128)(2,1)S(1)}, bf16[1,256,512]{2,1,0:T(8,128)(2,1)S(1)}, u32[]{:S(2)}, u32[]{:S(2)}) collective-permute-start(bf16[1,256,512]{2,1,0:T(8,128)(2,1)S(1)} %get-tuple-element.26), channel_id=1, source_target_pairs={{0,7},{1,6},{2,5},{3,4},{4,3},{5,2},{6,1},{7,0},{8,15},{9,14},{10,... | collective-permute-start | bytes 786440 | tf_op jit(solution)/shard_map/ppermute | solution.py:434
  252.5 2.4 collective-permute-done.8
  254.9 5.3 %collective-permute-start.11 = (bf16[1,256,512]{2,1,0:T(8,128)(2,1)S(1)}, bf16[1,256,512]{2,1,0:T(8,128)(2,1)S(1)}, u32[]{:S(2)}, u32[]{:S(2)}) collective-permute-start(bf16[1,256,512]{2,1,0:T(8,128)(2,1)S(1)} %get-tuple-element.28), channel_id=1, source_target_pairs={{0,5},{1,4},{2,7},{3,6},{4,1},{5,0},{6,3},{7,2},{8,13},{9,12},{10,... | collective-permute-start | bytes 786440 | tf_op jit(solution)/shard_map/ppermute | solution.py:434
  261.2 6.6 %collective-permute-done.9 = bf16[1,256,512]{2,1,0:T(8,128)(2,1)S(1)} collective-permute-done((bf16[1,256,512]{2,1,0:T(8,128)(2,1)}, bf16[1,256,512]{2,1,0:T(8,128)(2,1)S(1)}, u32[]{:S(2)}, u32[]{:S(2)}) %collective-permute-start.9) | collective-permute-done | bytes 262176 | tf_op jit(solution)/shard_map/ppermute | solution.py:434
  267.8 4.7 %collective-permute-done.10 = bf16[1,256,512]{2,1,0:T(8,128)(2,1)S(1)} collective-permute-done((bf16[1,256,512]{2,1,0:T(8,128)(2,1)S(1)}, bf16[1,256,512]{2,1,0:T(8,128)(2,1)S(1)}, u32[]{:S(2)}, u32[]{:S(2)}) %collective-permute-start.10) | collective-permute-done | bytes 262176 | tf_op jit(solution)/shard_map/ppermute | solution.py:434
  272.6 6.5 %collective-permute-done.11 = bf16[1,256,512]{2,1,0:T(8,128)(2,1)S(1)} collective-permute-done((bf16[1,256,512]{2,1,0:T(8,128)(2,1)S(1)}, bf16[1,256,512]{2,1,0:T(8,128)(2,1)S(1)}, u32[]{:S(2)}, u32[]{:S(2)}) %collective-permute-start.11) | collective-permute-done | bytes 262176 | tf_op jit(solution)/shard_map/ppermute | solution.py:434
  281.1 2.6 collective-permute-start.15
  284.6 2.7 collective-permute-start.16
  287.3 11.2 %counts.1 = f32[2,2048]{1,0:T(2,128)} custom-call(s32[2,8,16,128]{3,2,1,0:T(8,128)} %constant_dynamic-update-slice_fusion.ids_ref, f32[2,2048]{1,0:T(2,128)} %ema_ref.1, f32[2]{0:T(128)} %decay_ref.3), custom_call_target="tpu_custom_call" | custom-call | flops 4294967296 | bytes 262144 | tf_op jit(solution)/shard_map/counts/pallas_call | solution.py:321
  298.5 5.3 %collective-permute-done.17.refs_4_ = bf16[8,32,512]{2,1,0:T(8,128)(2,1)S(1)} collective-permute-done((bf16[8,32,512]{2,1,0:T(8,128)(2,1)S(1)}, bf16[8,32,512]{2,1,0:T(8,128)(2,1)S(1)}, u32[]{:S(2)}, u32[]{:S(2)}) %collective-permute-start.17) | collective-permute-done | bytes 262176 | tf_op jit(solution)/shard_map/ppermute | solution.py:421
  303.9 2.4 collective-permute-done.16.refs_3_
  307.4 5.0 %unpack.1 = bf16[1024,512]{1,0:T(8,128)(2,1)} custom-call(s32[2,1,512]{2,1,0:T(1,128)} %bitcast.43, bf16[8,64,512]{2,1,0:T(8,128)(2,1)} %get-tuple-element.25.refs_0_, bf16[8,64,512]{2,1,0:T(8,128)(2,1)} %copy-done.12, bf16[8,64,512]{2,1,0:T(8,128)(2,1)} %copy-done.11, bf16[8,32,512]{2,1,0:T(8,128)(2,1)} %copy-done.16, bf16[8,32,512]{2,1,0:T(8,128)(2,1)} %copy-done.14), custom_call_target="tpu_custom_call" | custom-call | flops 2147483648 | bytes 3145728 | tf_op jit(solution)/shard_map/unpack/pallas_call | solution.py:148
  314.6 9.1 %sums.2.rest_0_ = f32[2,64,2048]{2,1,0:T(8,128)} custom-call(bf16[256,32,128]{2,1,0:T(8,128)(2,1)} %all-to-all-done.3.got_ref, s32[2,8,16,128]{3,2,1,0:T(8,128)} %constant_dynamic-update-slice_fusion.ids_ref, f32[2,64,2048]{2,1,0:T(8,128)} %bitcast.44, f32[2]{0:T(128)} %decay_ref.3), custom_call_target="tpu_custom_call" | custom-call | flops 4294967296 | bytes 4194304 | tf_op jit(solution)/shard_map/sums/pallas_call | solution.py:396
  323.7 9.1 %sums.3 = f32[2,64,2048]{2,1,0:T(8,128)} custom-call(bf16[256,32,128]{2,1,0:T(8,128)(2,1)} %all-to-all-done.2.got_ref, s32[2,8,16,128]{3,2,1,0:T(8,128)} %constant_dynamic-update-slice_fusion.ids_ref, f32[2,64,2048]{2,1,0:T(8,128)} %bitcast.45, f32[2]{0:T(128)} %decay_ref.3, f32[2,64,2048]{2,1,0:T(8,128)} %sums.2.rest_0_), custom_call_target="tpu_custom_call", output_to_operand_aliasing={{}: (4, {})} | custom-call | flops 4294967296 | bytes 4194304 | tf_op jit(solution)/shard_map/sums/pallas_call | solution.py:396
  (89 shorter events, 29.2 us)
Async XLA Ops:
  0.6 9.0 %copy-start.3 = (s32[2,2,2,128]{3,2,1,0:T(2,128)S(1)}, s32[2,2,2,128]{3,2,1,0:T(2,128)}, u32[]{:S(2)}) copy-start(s32[2,2,2,128]{3,2,1,0:T(2,128)} %param.19) | copy-start | bytes 12292
  0.6 9.0 %copy-start.4 = (s32[2,2,2,128]{3,2,1,0:T(2,128)S(1)}, s32[2,2,2,128]{3,2,1,0:T(2,128)}, u32[]{:S(2)}) copy-start(s32[2,2,2,128]{3,2,1,0:T(2,128)} %param.18) | copy-start | bytes 12292
  2.0 24.8 %collective-permute-start.1 = (bf16[2,2,128,512]{3,2,1,0:T(8,128)(2,1)S(1)}, bf16[2,2,128,512]{3,2,1,0:T(8,128)(2,1)S(1)}, u32[]{:S(2)}, u32[]{:S(2)}) collective-permute-start(bf16[2,2,128,512]{3,2,1,0:T(8,128)(2,1)S(1)} %get-tuple-element.39), channel_id=1, source_target_pairs={{1,0},{2,1},{3,2},{4,3},{5,4},{6,5},{7,6},{8,7},{9,8},{10,9},{11,1... | collective-permute-start | bytes 1572872 | tf_op jit(solution)/shard_map/ppermute | solution.py:468
  7.1 19.7 %collective-permute-start = (bf16[2,2,128,512]{3,2,1,0:T(8,128)(2,1)S(1)}, bf16[2,2,128,512]{3,2,1,0:T(8,128)(2,1)S(1)}, u32[]{:S(2)}, u32[]{:S(2)}) collective-permute-start(bf16[2,2,128,512]{3,2,1,0:T(8,128)(2,1)S(1)} %get-tuple-element.40), channel_id=1, source_target_pairs={{0,1},{1,2},{2,3},{3,4},{4,5},{5,6},{6,7},{7,8},{8,9},{9,10},{10,1... | collective-permute-start | bytes 1572872 | tf_op jit(solution)/shard_map/ppermute | solution.py:467
  13.9 23.3 %all-to-all-start = ((s32[64,1,128]{2,1,0:T(1,128)}), s32[64,1,128]{2,1,0:T(1,128)S(1)}, u32[]{:S(2)}, u32[]{:S(2)}) async-start(s32[64,1,128]{2,1,0:T(1,128)} %bitcast.4), calls=%async_computation | async-start | bytes 65536 | tf_op jit(solution)/shard_map/all_to_all | solution.py:475
  45.7 5.0 %copy-start.5 = (bf16[4,256,512]{2,1,0:T(8,128)(2,1)S(1)}, bf16[4,256,512]{2,1,0:T(8,128)(2,1)}, u32[]{:S(2)}) copy-start(bf16[4,256,512]{2,1,0:T(8,128)(2,1)} %conv.1) | copy-start | bytes 3145732
  45.8 12.1 %copy-start.1 = (s32[2,1024]{1,0:T(2,128)S(1)}, s32[2,1024]{1,0:T(2,128)}, u32[]{:S(2)}) copy-start(s32[2,1024]{1,0:T(2,128)} %get-tuple-element.15) | copy-start | bytes 24580
  45.8 12.2 %copy-start.2 = (s32[2,1024]{1,0:T(2,128)S(1)}, s32[2,1024]{1,0:T(2,128)}, u32[]{:S(2)}) copy-start(s32[2,1024]{1,0:T(2,128)} %get-tuple-element.17) | copy-start | bytes 24580
  45.8 58.7 %all-to-all-start.1 = ((bf16[8,256,512]{2,1,0:T(8,128)(2,1)}), bf16[8,256,512]{2,1,0:T(8,128)(2,1)S(1)}, u32[]{:S(2)}, u32[]{:S(2)}) async-start(bf16[8,256,512]{2,1,0:T(8,128)(2,1)} %serve.2), calls=%async_computation.1 | async-start | bytes 4194304 | tf_op jit(solution)/shard_map/all_to_all | solution.py:426
  50.7 44.2 %collective-permute-start.2 = (bf16[4,256,512]{2,1,0:T(8,128)(2,1)S(1)}, bf16[4,256,512]{2,1,0:T(8,128)(2,1)S(1)}, u32[]{:S(2)}, u32[]{:S(2)}) collective-permute-start(bf16[4,256,512]{2,1,0:T(8,128)(2,1)S(1)} %copy-done.5), channel_id=1, source_target_pairs={{0,32},{32,64},{64,96},{96,128},{128,160},{160,192},{192,224},{1,3... | collective-permute-start | bytes 3145736 | tf_op jit(solution)/shard_map/ppermute | solution.py:479
  104.5 101.3 %all-to-all-start.3 = ((bf16[256,32,128]{2,1,0:T(8,128)(2,1)}), bf16[256,32,128]{2,1,0:T(8,128)(2,1)}, u32[]{:S(2)}, u32[]{:S(2)}) async-start(bf16[256,32,128]{2,1,0:T(8,128)(2,1)} %bitcast.35), calls=%async_computation.3 | async-start | bytes 4194304 | tf_op jit(solution)/shard_map/all_to_all | solution.py:449
  127.8 66.7 %collective-permute-start.4 = (bf16[8,64,512]{2,1,0:T(8,128)(2,1)S(1)}, bf16[8,64,512]{2,1,0:T(8,128)(2,1)S(1)}, u32[]{:S(2)}, u32[]{:S(2)}) collective-permute-start(bf16[8,64,512]{2,1,0:T(8,128)(2,1)S(1)} %get-tuple-element.36), channel_id=1, source_target_pairs={{0,56},{1,57},{2,58},{3,59},{4,60},{5,61},{6,62},{7,63},{8,0},{9,1... | collective-permute-start | bytes 1572872 | tf_op jit(solution)/shard_map/ppermute | solution.py:421
  132.1 62.4 %collective-permute-start.3 = (bf16[8,64,512]{2,1,0:T(8,128)(2,1)S(1)}, bf16[8,64,512]{2,1,0:T(8,128)(2,1)S(1)}, u32[]{:S(2)}, u32[]{:S(2)}) collective-permute-start(bf16[8,64,512]{2,1,0:T(8,128)(2,1)S(1)} %get-tuple-element.37), channel_id=1, source_target_pairs={{0,8},{1,9},{2,10},{3,11},{4,12},{5,13},{6,14},{7,15},{8,16},{9,17... | collective-permute-start | bytes 1572872 | tf_op jit(solution)/shard_map/ppermute | solution.py:421
  132.1 60.5 %collective-permute-start.6 = (bf16[8,32,512]{2,1,0:T(8,128)(2,1)S(1)}, bf16[8,32,512]{2,1,0:T(8,128)(2,1)S(1)}, u32[]{:S(2)}, u32[]{:S(2)}) collective-permute-start(bf16[8,32,512]{2,1,0:T(8,128)(2,1)S(1)} %get-tuple-element.34), channel_id=1, source_target_pairs={{0,16},{1,17},{2,18},{3,19},{4,20},{5,21},{6,22},{7,23},{8,24},{9,... | collective-permute-start | bytes 786440 | tf_op jit(solution)/shard_map/ppermute | solution.py:421
  132.2 62.3 %collective-permute-start.5 = (bf16[8,32,512]{2,1,0:T(8,128)(2,1)S(1)}, bf16[8,32,512]{2,1,0:T(8,128)(2,1)S(1)}, u32[]{:S(2)}, u32[]{:S(2)}) collective-permute-start(bf16[8,32,512]{2,1,0:T(8,128)(2,1)S(1)} %get-tuple-element.35), channel_id=1, source_target_pairs={{0,48},{1,49},{2,50},{3,51},{4,52},{5,53},{6,54},{7,55},{8,56},{9,... | collective-permute-start | bytes 786440 | tf_op jit(solution)/shard_map/ppermute | solution.py:421
  192.7 1.8 copy-start.13
  194.5 1.1 copy-start.10
  205.8 117.9 %all-to-all-start.2 = ((bf16[256,32,128]{2,1,0:T(8,128)(2,1)}), bf16[256,32,128]{2,1,0:T(8,128)(2,1)}, u32[]{:S(2)}, u32[]{:S(2)}) async-start(bf16[256,32,128]{2,1,0:T(8,128)(2,1)} %bitcast.34), calls=%async_computation.2 | async-start | bytes 4194304 | tf_op jit(solution)/shard_map/all_to_all | solution.py:449
  230.3 19.6 %collective-permute-start.7 = (bf16[1,256,512]{2,1,0:T(8,128)(2,1)}, bf16[1,256,512]{2,1,0:T(8,128)(2,1)}, u32[]{:S(2)}, u32[]{:S(2)}) collective-permute-start(bf16[1,256,512]{2,1,0:T(8,128)(2,1)} %get-tuple-element.32), channel_id=1, source_target_pairs={{0,1},{1,0},{2,3},{3,2},{4,5},{5,4},{6,7},{7,6},{8,9},{9,8},{10,11... | collective-permute-start | bytes 786440 | tf_op jit(solution)/shard_map/ppermute | solution.py:434
  243.5 11.4 %collective-permute-start.8 = (bf16[1,256,512]{2,1,0:T(8,128)(2,1)}, bf16[1,256,512]{2,1,0:T(8,128)(2,1)}, u32[]{:S(2)}, u32[]{:S(2)}) collective-permute-start(bf16[1,256,512]{2,1,0:T(8,128)(2,1)} %get-tuple-element.31), channel_id=1, source_target_pairs={{0,2},{1,3},{2,0},{3,1},{4,6},{5,7},{6,4},{7,5},{8,10},{9,11},{10,... | collective-permute-start | bytes 786440 | tf_op jit(solution)/shard_map/ppermute | solution.py:434
  244.3 35.8 %collective-permute-start.13 = (bf16[1,256,512]{2,1,0:T(8,128)(2,1)S(1)}, bf16[1,256,512]{2,1,0:T(8,128)(2,1)S(1)}, u32[]{:S(2)}, u32[]{:S(2)}) collective-permute-start(bf16[1,256,512]{2,1,0:T(8,128)(2,1)S(1)} %get-tuple-element.26), channel_id=1, source_target_pairs={{0,7},{1,6},{2,5},{3,4},{4,3},{5,2},{6,1},{7,0},{8,15},{9,14},{10,... | collective-permute-start | bytes 786440 | tf_op jit(solution)/shard_map/ppermute | solution.py:434
  247.8 32.2 %collective-permute-start.12 = (bf16[1,256,512]{2,1,0:T(8,128)(2,1)S(1)}, bf16[1,256,512]{2,1,0:T(8,128)(2,1)S(1)}, u32[]{:S(2)}, u32[]{:S(2)}) collective-permute-start(bf16[1,256,512]{2,1,0:T(8,128)(2,1)S(1)} %get-tuple-element.27), channel_id=1, source_target_pairs={{0,6},{1,7},{2,4},{3,5},{4,2},{5,3},{6,0},{7,1},{8,14},{9,15},{10,... | collective-permute-start | bytes 786440 | tf_op jit(solution)/shard_map/ppermute | solution.py:434
  249.3 18.5 %collective-permute-start.9 = (bf16[1,256,512]{2,1,0:T(8,128)(2,1)}, bf16[1,256,512]{2,1,0:T(8,128)(2,1)S(1)}, u32[]{:S(2)}, u32[]{:S(2)}) collective-permute-start(bf16[1,256,512]{2,1,0:T(8,128)(2,1)} %get-tuple-element.30), channel_id=1, source_target_pairs={{0,3},{1,2},{2,1},{3,0},{4,7},{5,6},{6,5},{7,4},{8,11},{9,10},{10,... | collective-permute-start | bytes 786440 | tf_op jit(solution)/shard_map/ppermute | solution.py:434
  250.0 22.6 %collective-permute-start.10 = (bf16[1,256,512]{2,1,0:T(8,128)(2,1)S(1)}, bf16[1,256,512]{2,1,0:T(8,128)(2,1)S(1)}, u32[]{:S(2)}, u32[]{:S(2)}) collective-permute-start(bf16[1,256,512]{2,1,0:T(8,128)(2,1)S(1)} %get-tuple-element.29), channel_id=1, source_target_pairs={{0,4},{1,5},{2,6},{3,7},{4,0},{5,1},{6,2},{7,3},{8,12},{9,13},{10,... | collective-permute-start | bytes 786440 | tf_op jit(solution)/shard_map/ppermute | solution.py:434
  254.9 24.1 %collective-permute-start.11 = (bf16[1,256,512]{2,1,0:T(8,128)(2,1)S(1)}, bf16[1,256,512]{2,1,0:T(8,128)(2,1)S(1)}, u32[]{:S(2)}, u32[]{:S(2)}) collective-permute-start(bf16[1,256,512]{2,1,0:T(8,128)(2,1)S(1)} %get-tuple-element.28), channel_id=1, source_target_pairs={{0,5},{1,4},{2,7},{3,6},{4,1},{5,0},{6,3},{7,2},{8,13},{9,12},{10,... | collective-permute-start | bytes 786440 | tf_op jit(solution)/shard_map/ppermute | solution.py:434
  281.1 25.2 %collective-permute-start.15 = (bf16[8,64,512]{2,1,0:T(8,128)(2,1)S(1)}, bf16[8,64,512]{2,1,0:T(8,128)(2,1)S(1)}, u32[]{:S(2)}, u32[]{:S(2)}) collective-permute-start(bf16[8,64,512]{2,1,0:T(8,128)(2,1)S(1)} %get-tuple-element.23), channel_id=1, source_target_pairs={{0,56},{1,57},{2,58},{3,59},{4,60},{5,61},{6,62},{7,63},{8,0},{9,1... | collective-permute-start | bytes 1572872 | tf_op jit(solution)/shard_map/ppermute | solution.py:421
  283.6 22.6 %collective-permute-start.14 = (bf16[8,64,512]{2,1,0:T(8,128)(2,1)S(1)}, bf16[8,64,512]{2,1,0:T(8,128)(2,1)S(1)}, u32[]{:S(2)}, u32[]{:S(2)}) collective-permute-start(bf16[8,64,512]{2,1,0:T(8,128)(2,1)S(1)} %get-tuple-element.24), channel_id=1, source_target_pairs={{0,8},{1,9},{2,10},{3,11},{4,12},{5,13},{6,14},{7,15},{8,16},{9,17... | collective-permute-start | bytes 1572872 | tf_op jit(solution)/shard_map/ppermute | solution.py:421
  283.7 20.2 %collective-permute-start.17 = (bf16[8,32,512]{2,1,0:T(8,128)(2,1)S(1)}, bf16[8,32,512]{2,1,0:T(8,128)(2,1)S(1)}, u32[]{:S(2)}, u32[]{:S(2)}) collective-permute-start(bf16[8,32,512]{2,1,0:T(8,128)(2,1)S(1)} %get-tuple-element.21), channel_id=1, source_target_pairs={{0,16},{1,17},{2,18},{3,19},{4,20},{5,21},{6,22},{7,23},{8,24},{9,... | collective-permute-start | bytes 786440 | tf_op jit(solution)/shard_map/ppermute | solution.py:421
  284.6 21.6 %collective-permute-start.16 = (bf16[8,32,512]{2,1,0:T(8,128)(2,1)S(1)}, bf16[8,32,512]{2,1,0:T(8,128)(2,1)S(1)}, u32[]{:S(2)}, u32[]{:S(2)}) collective-permute-start(bf16[8,32,512]{2,1,0:T(8,128)(2,1)S(1)} %get-tuple-element.22), channel_id=1, source_target_pairs={{0,48},{1,49},{2,50},{3,51},{4,52},{5,53},{6,54},{7,55},{8,56},{9,... | collective-permute-start | bytes 786440 | tf_op jit(solution)/shard_map/ppermute | solution.py:421
  303.9 2.4 copy-start.14
  306.2 1.1 copy-start.12
  307.4 5.0 %copy-start = (bf16[1024,512]{1,0:T(8,128)(2,1)S(1)}, bf16[1024,512]{1,0:T(8,128)(2,1)}, u32[]{:S(2)}) copy-start(bf16[1024,512]{1,0:T(8,128)(2,1)} %get-tuple-element.20) | copy-start | bytes 3145732
  (7 other events, 5.9 us)
